TPU v7x, 32 devices: a 4x4x1 block of a 4x4x8 slice. The times are simulated.
32 devices in a mesh: dp: 1 (over z), tp: 32 (over x, y, core).
Axes of the slice: x: 4, y: 4, z: 1, core: 2. Of those that a mesh axis runs over, the one named last changes fastest.
The devices are a block of a 4x4x8 slice.
Arguments:
- x: bfloat16 [2048, 8192], P('dp')
- w_gate: bfloat16 [8192, 49152], P(None, 'tp')
- w_up: bfloat16 [8192, 49152], P(None, 'tp')
- w_down: bfloat16 [49152, 8192], P('tp')
Outputs:
- output: bfloat16 [2048, 8192], P('dp')
All inputs are finite; a program needn't handle non-finite values.
Results may differ from a plain program's by a relative error of at most 0.016.
Values are sent between devices in bfloat16 or wider.
A program may use at most 768 MiB of HBM per device.

v0:
```python
import jax
import jax.numpy as jnp
from jax import lax
from jax.sharding import PartitionSpec as P


def solution(mesh):
    def step(x, w_gate, w_up, w_down):
        gate = jnp.dot(x, w_gate, preferred_element_type=jnp.float32)
        up = jnp.dot(x, w_up, preferred_element_type=jnp.float32)
        hidden = (jax.nn.silu(gate) * up).astype(jnp.bfloat16)
        term = jnp.dot(hidden, w_down, preferred_element_type=jnp.float32).astype(jnp.bfloat16)
        return lax.psum(term, "tp")

    return jax.shard_map(
        step,
        mesh=mesh,
        in_specs=(P("dp", None), P(None, "tp"), P(None, "tp"), P("tp", None)),
        out_specs=P("dp", None),
        check_vma=False,
    )
```

profile of v0, /device:TPU:97, one launch (start us, length us, event | category | flops | bytes accessed | tf_op | source)
XLA Modules:
  0.0 473.7 jit_solution(10010676465742393320)
XLA Ops:
  6.5 0.0 all-reduce.2.cloned.1.call-start
  6.6 60.4 %fusion = f32[2048,1536]{1,0:T(8,128)} fusion(bf16[2048,8192]{1,0:T(8,128)(2,1)} %param.4, bf16[8192,1536]{1,0:T(8,128)(2,1)} %param.5), kind=kOutput, calls=%fused_computation.2 | convolution fusion | flops 51539607552 | bytes 71303168 | tf_op jit(solution)/shard_map/dot_general | solution.py:9
  67.0 63.4 %multiply_convert_fusion = bf16[2048,1536]{1,0:T(8,128)(2,1)S(1)} fusion(f32[2048,1536]{1,0:T(8,128)} %fusion, bf16[2048,8192]{1,0:T(8,128)(2,1)} %param.4, bf16[8192,1536]{1,0:T(8,128)(2,1)} %param.6), kind=kOutput, calls=%fused_computation.1 | convolution fusion | flops 51558481920 | bytes 77594624 | tf_op jit(solution)/shard_map/dot_general | solution.py:10
  130.4 60.1 %convolution_convert_fusion = bf16[2048,8192]{1,0:T(8,128)(2,1)} fusion(bf16[2048,1536]{1,0:T(8,128)(2,1)S(1)} %multiply_convert_fusion, bf16[1536,8192]{1,0:T(8,128)(2,1)} %param.7), kind=kOutput, calls=%fused_computation | convolution fusion | flops 51556384768 | bytes 65011712 | tf_op jit(solution)/shard_map/dot_general | solution.py:12
  190.5 0.1 all-reduce.2.cloned.1.call-update
  190.6 253.3 %all-reduce.2.cloned.1.call-done = bf16[2048,8192]{1,0:T(8,128)(2,1)} async-done(((bf16[2048,8192]{1,0:T(8,128)(2,1)}), bf16[2048,8192]{1,0:T(8,128)(2,1)}) %all-reduce.2.cloned.1.call-update) | async-done | bytes 33554448 | tf_op jit(solution)/shard_map/psum | solution.py:13
  443.9 23.0 %copy.6 = bf16[2048,8192]{1,0:T(8,128)(2,1)} copy(bf16[2048,8192]{1,0:T(8,128)(2,1)} %all-reduce.2.cloned.1.call-done) | data formatting | bytes 67108864
Async XLA Ops:
  6.5 437.3 %all-reduce.2.cloned.1.call-start = ((), (), s32[]{:S(2)}) async-start(), calls=%async_computation | async-start | bytes 67108864 | tf_op jit(solution)/shard_map/psum | solution.py:13
Sparse Core Ops, SparseCore 0:
  190.7 253.1 all-reduce.1
where the time goes:
time: 474 us
  waiting for transfers between devices  253 us (53%)
  matrix products  184 us (39%)
  local copies, waits for them, and re-layouts  23 us (5%)
  between operations  13.4 us (3%)
    psum x1, waiting for transfers between devices, step(): return lax.psum(term, 'tp')  253 us
    dot_general x1, matrix products, step(): up = jnp.dot(x, w_up, preferred_element_type=jnp.float32)  63.4 us
    dot_general x1, matrix products, step(): gate = jnp.dot(x, w_gate, preferred_element_type=jnp.float32)  60.4 us
    dot_general x1, matrix products, step(): jnp.dot(hidden, w_down, preferred_element_type=jnp.float32)  60.1 us
    unnamed x1, local copies, waits for them, and re-layouts  23 us
  transfers between devices with their start and end apart: 1, of which 1 were waited for; matrix products, arithmetic and copies ran while one was open for 0% of the time, Pallas kernels for 0%

commit v1 on v0

v1 whole, which is shorter than its diff:
```python
import functools
import math

import jax
import jax.numpy as jnp
from jax import lax
from jax.experimental import pallas as pl
from jax.experimental.pallas import tpu as pltpu
from jax.sharding import PartitionSpec as P

AXIS = "tp"
CORES = 2
RING = 4
STREAMS = 2
CHUNK = 512
FF_TILE = 256
UNITS = 4
TILES = 2
SLOTS = 4
FIRST = 15
OFFSETS = (0, 3, 5, 7, 9, 11, 13, 16, 18)
VMEM_LIMIT = 67_043_328


def _kernel(
    cfg, x_hbm, wg_hbm, wu_hbm, wd_hbm, y_hbm,
    x_v, h_v, wg_v, wu_v, wd_v, own, psend, precv, s1, r1, s2, r2, f1, fin,
    x_sem, wg_sem, wu_sem, wd_sem, pair_ss, pair_rs, s1_ss, s1_rs, s2_ss, s2_rs,
    g2_ss, g2_rs, g1_ss, g1_rs, loc_sem, share_ss, share_rs, credit,
):
    side, rows, chunk, ff_tile, unit = cfg
    n_chunks = rows // chunk
    n_units = n_chunks * UNITS
    n_ff = h_v.shape[1] // ff_tile
    gu_ticks = 2 * n_ff
    down_ticks = UNITS * TILES
    per_chunk = gu_ticks + down_ticks
    pace = per_chunk // UNITS
    tile = unit // TILES
    half_rows = chunk // CORES
    srows = half_rows // STREAMS
    brows = srows // RING
    bcols = unit // RING
    h1 = unit // 2
    h2 = bcols // 2
    xpiece = chunk // down_ticks

    me = lax.axis_index(AXIS)
    core = lax.rem(me, CORES)
    chip = lax.div(me, CORES)
    cx, cy = lax.div(chip, side), lax.rem(chip, side)

    def at(px, py):
        return (px * side + py) * CORES + core

    nxt = lambda v: lax.rem(v + 1, side)
    prv = lambda v: lax.rem(v + side - 1, side)
    xp, xm, yp, ym = at(nxt(cx), cy), at(prv(cx), cy), at(cx, nxt(cy)), at(cx, prv(cy))
    partner = chip * CORES + (1 - core)
    pos1, pos2 = (cx, cy), (cy, cx)
    ring1, ring2 = ((xp, xm), (yp, ym)), ((yp, ym), (xp, xm))

    bar = pltpu.get_barrier_semaphore()
    for d in (xp, xm, yp, ym, partner):
        pl.semaphore_signal(bar, inc=1, device_id={AXIS: d}, device_id_type=pl.DeviceIdType.MESH)
    pl.semaphore_wait(bar, 5)

    def remote(src, dst, ss, rs, dev):
        return pltpu.make_async_remote_copy(
            src_ref=src, dst_ref=dst, send_sem=ss, recv_sem=rs,
            device_id={AXIS: dev}, device_id_type=pl.DeviceIdType.MESH,
        )

    def w_copies(g):
        slot = lax.rem(g, 2)
        cols = pl.ds(pl.multiple_of(lax.rem(g, n_ff) * ff_tile, ff_tile), ff_tile)
        return (
            pltpu.make_async_copy(wg_hbm.at[:, cols], wg_v.at[slot], wg_sem.at[slot]),
            pltpu.make_async_copy(wu_hbm.at[:, cols], wu_v.at[slot], wu_sem.at[slot]),
        )

    def wd_copy(g):
        slot = lax.rem(g, 2)
        cols = pl.ds(pl.multiple_of(lax.rem(g, down_ticks) * tile, tile), tile)
        return pltpu.make_async_copy(wd_hbm.at[:, cols], wd_v.at[slot], wd_sem.at[slot])

    def x_copy(c, i):
        src = pl.ds(pl.multiple_of(c * chunk + i * xpiece, xpiece), xpiece)
        dst = pl.ds(pl.multiple_of(i * xpiece, xpiece), xpiece)
        return pltpu.make_async_copy(x_hbm.at[src], x_v.at[dst], x_sem.at[i])

    def pair_copy(u):
        ps, s = lax.rem(u, 2), lax.rem(u, SLOTS)
        return remote(psend.at[ps], precv.at[s], pair_ss.at[ps], pair_rs.at[s], partner)

    def rs_copy(ring, u, st, k):
        s = lax.rem(u, SLOTS)
        if ring == 1:
            sb, rb, ss, rs, nb = s1, r1, s1_ss, s1_rs, ring1
        else:
            sb, rb, ss, rs, nb = s2, r2, s2_ss, s2_rs, ring2
        return remote(sb.at[s, st, k], rb.at[s, st, k], ss.at[s, st, k], rs.at[s, st, k], nb[st][k % 2])

    def y_rows(u, st, q):
        base = lax.div(u, UNITS) * chunk + core * half_rows + st * srows + q * brows
        return pl.ds(pl.multiple_of(base, brows), brows)

    def y_cols(u, off, width):
        return pl.ds(pl.multiple_of(lax.rem(u, UNITS) * unit + off, width), width)

    def ag2_copy(u, st, k):
        s = lax.rem(u, SLOTS)
        p1, p2 = pos1[st], pos2[st]
        if k < 2:
            dst = y_hbm.at[y_rows(u, st, p1), y_cols(u, p2 * bcols, bcols)]
            src = fin.at[s, st]
        else:
            off = prv(p2) * bcols if k == 2 else nxt(p2) * bcols + h2
            src = dst = y_hbm.at[y_rows(u, st, p1), y_cols(u, off, h2)]
        return remote(src, dst, g2_ss.at[s, st, k], g2_rs.at[s, st, k], ring2[st][k % 2])

    def loc_copy(u, st):
        s = lax.rem(u, SLOTS)
        dst = y_hbm.at[y_rows(u, st, pos1[st]), y_cols(u, pos2[st] * bcols, bcols)]
        return pltpu.make_async_copy(fin.at[s, st], dst, loc_sem.at[s, st])

    def ag1_copy(u, st, k):
        s = lax.rem(u, SLOTS)
        p1 = pos1[st]
        if k < 2:
            part = y_hbm.at[y_rows(u, st, p1), y_cols(u, 0, unit)]
        elif k == 2:
            part = y_hbm.at[y_rows(u, st, prv(p1)), y_cols(u, 0, h1)]
        else:
            part = y_hbm.at[y_rows(u, st, nxt(p1)), y_cols(u, h1, h1)]
        return remote(part, part, g1_ss.at[s, st, k], g1_rs.at[s, st, k], ring1[st][k % 2])

    def share_copy(u):
        base = lax.div(u, UNITS) * chunk + core * half_rows
        part = y_hbm.at[pl.ds(pl.multiple_of(base, half_rows), half_rows), y_cols(u, 0, unit)]
        return remote(part, part, share_ss.at[u], share_rs.at[u], partner)

    f32 = lambda v: v.astype(jnp.float32)
    b16 = lambda v: v.astype(jnp.bfloat16)
    A1, B1 = pl.ds(0, h1), pl.ds(h1, h1)

    def rows_of(st, q):
        return pl.ds(pl.multiple_of(st * srows + q * brows, brows), brows)

    def stage_pair(u):
        s = lax.rem(u, SLOTS)
        pair_copy(u).wait_recv()
        for st in range(STREAMS):
            p = pos1[st]
            for d, cols, k in (
                (2, A1, 0), (2, B1, 1), (1, B1, 2), (3, A1, 3),
                (1, A1, None), (3, B1, None), (0, A1, None), (0, B1, None),
            ):
                r = rows_of(st, lax.rem(p + d, side))
                v = own[s, r, cols] + f32(precv[s, r, cols])
                if k is None:
                    own[s, r, cols] = v
                else:
                    s1[s, st, k] = b16(v)
        for k in range(4):
            for st in range(STREAMS):
                rs_copy(1, u, st, k).start()

        @pl.when(u + SLOTS < n_units)
        def _():
            pl.semaphore_signal(credit, inc=1, device_id={AXIS: partner}, device_id_type=pl.DeviceIdType.MESH)

    def stage_rs1_fwd(u):
        s = lax.rem(u, SLOTS)
        for st in range(STREAMS):
            p = pos1[st]
            rs_copy(1, u, st, 0).wait_recv()
            s1[s, st, 4] = b16(own[s, rows_of(st, nxt(p)), A1] + f32(r1[s, st, 0]))
            rs_copy(1, u, st, 1).wait_recv()
            s1[s, st, 5] = b16(own[s, rows_of(st, prv(p)), B1] + f32(r1[s, st, 1]))
        for k in (4, 5):
            for st in range(STREAMS):
                rs_copy(1, u, st, k).start()

    def stage_rs1_end(u):
        s = lax.rem(u, SLOTS)
        fs = lax.rem(u, 2)
        for st in range(STREAMS):
            r = rows_of(st, pos1[st])
            for k in (3, 4, 2, 5):
                rs_copy(1, u, st, k).wait_recv()
            f1[fs, st, :, A1] = own[s, r, A1] + f32(r1[s, st, 3]) + f32(r1[s, st, 4])
            f1[fs, st, :, B1] = own[s, r, B1] + f32(r1[s, st, 2]) + f32(r1[s, st, 5])
            for d, off, k in ((2, 0, 0), (2, h2, 1), (1, h2, 2), (3, 0, 3)):
                q = lax.rem(pos2[st] + d, side)
                s2[s, st, k] = b16(f1[fs, st, :, pl.ds(pl.multiple_of(q * bcols + off, h2), h2)])
        for k in range(4):
            for st in range(STREAMS):
                rs_copy(2, u, st, k).start()

    def f1_half(u, st, q, off):
        return f1[lax.rem(u, 2), st, :, pl.ds(pl.multiple_of(q * bcols + off, h2), h2)]

    def stage_rs2_fwd(u):
        s = lax.rem(u, SLOTS)
        for st in range(STREAMS):
            p = pos2[st]
            rs_copy(2, u, st, 0).wait_recv()
            s2[s, st, 4] = b16(f1_half(u, st, nxt(p), 0) + f32(r2[s, st, 0]))
            rs_copy(2, u, st, 1).wait_recv()
            s2[s, st, 5] = b16(f1_half(u, st, prv(p), h2) + f32(r2[s, st, 1]))
        for k in (4, 5):
            for st in range(STREAMS):
                rs_copy(2, u, st, k).start()

    def stage_rs2_end(u):
        s = lax.rem(u, SLOTS)
        for st in range(STREAMS):
            p = pos2[st]
            for k in (3, 4, 2, 5):
                rs_copy(2, u, st, k).wait_recv()
            a = f1_half(u, st, p, 0) + f32(r2[s, st, 3]) + f32(r2[s, st, 4])
            b = f1_half(u, st, p, h2) + f32(r2[s, st, 2]) + f32(r2[s, st, 5])
            fin[s, st, :, pl.ds(0, h2)] = b16(a)
            fin[s, st, :, pl.ds(h2, h2)] = b16(b)
        for st in range(STREAMS):
            for k in range(2):
                ag2_copy(u, st, k).start()
            loc_copy(u, st).start()

    def stage_ag2_fwd(u):
        for st in range(STREAMS):
            for k in range(2):
                ag2_copy(u, st, k).wait_recv()
                ag2_copy(u, st, k + 2).start()

    def stage_ag1(u):
        for st in range(STREAMS):
            loc_copy(u, st).wait()
            for k in (2, 3):
                ag2_copy(u, st, k).wait_recv()
            for k in range(2):
                ag1_copy(u, st, k).start()

    def stage_ag1_fwd(u):
        for st in range(STREAMS):
            for k in range(2):
                ag1_copy(u, st, k).wait_recv()
                ag1_copy(u, st, k + 2).start()

    def stage_share(u):
        for st in range(STREAMS):
            for k in (2, 3):
                ag1_copy(u, st, k).wait_recv()
        share_copy(u).start()
        for st in range(STREAMS):
            for k in range(6):
                rs_copy(1, u, st, k).wait_send()
                rs_copy(2, u, st, k).wait_send()
            for k in range(4):
                ag2_copy(u, st, k).wait_send()
                ag1_copy(u, st, k).wait_send()

    stages = (
        stage_pair, stage_rs1_fwd, stage_rs1_end, stage_rs2_fwd, stage_rs2_end,
        stage_ag2_fwd, stage_ag1, stage_ag1_fwd, stage_share,
    )

    def gate_up(c, tc):
        f, mh = lax.div(tc, 2), lax.rem(tc, 2)
        g = c * n_ff + f
        slot = lax.rem(g, 2)

        @pl.when(mh == 0)
        def _():
            for cp in w_copies(g):
                cp.wait()

            @pl.when(g + 1 < n_chunks * n_ff)
            def _():
                for cp in w_copies(g + 1):
                    cp.start()

        @pl.when(tc < 2)
        def _():
            for i in range(down_ticks // 2):
                x_copy(c, mh * (down_ticks // 2) + i).wait()

        m = pl.ds(pl.multiple_of(mh * half_rows, half_rows), half_rows)
        gate = jnp.dot(x_v[m, :], wg_v[slot], preferred_element_type=jnp.float32)
        up = jnp.dot(x_v[m, :], wu_v[slot], preferred_element_type=jnp.float32)
        cols = pl.ds(pl.multiple_of(f * ff_tile, ff_tile), ff_tile)
        h_v[m, cols] = b16(jax.nn.silu(gate) * up)

    def down(c, n):
        g = c * down_ticks + n
        j, i = lax.div(n, TILES), lax.rem(n, TILES)
        u = c * UNITS + j
        s, ps = lax.rem(u, SLOTS), lax.rem(u, 2)
        slot = lax.rem(g, 2)
        wd_copy(g).wait()

        @pl.when(g + 1 < n_chunks * down_ticks)
        def _():
            wd_copy(g + 1).start()

        @pl.when(c + 1 < n_chunks)
        def _():
            x_copy(c + 1, n).start()

        @pl.when((i == 0) & (u >= 2))
        def _():
            pair_copy(u - 2).wait_send()

        cols = pl.ds(pl.multiple_of(i * tile, tile), tile)
        theirs = pl.ds(pl.multiple_of((1 - core) * half_rows, half_rows), half_rows)
        mine = pl.ds(pl.multiple_of(core * half_rows, half_rows), half_rows)
        psend[ps, :, cols] = b16(jnp.dot(h_v[theirs, :], wd_v[slot], preferred_element_type=jnp.float32))
        own[s, :, cols] = jnp.dot(h_v[mine, :], wd_v[slot], preferred_element_type=jnp.float32)

        @pl.when(i == TILES - 1)
        def _():
            @pl.when(u >= SLOTS)
            def _():
                pl.semaphore_wait(credit, 1)

            pair_copy(u).start()

    for i in range(down_ticks // 2):
        x_copy(0, i).start()
    for cp in w_copies(0):
        cp.start()
    for i in range(down_ticks // 2, down_ticks):
        x_copy(0, i).start()
    wd_copy(0).start()

    total = (n_units - 1) * pace + FIRST + OFFSETS[-1] + 1

    def tick(t, carry):
        c, tc = lax.div(t, per_chunk), lax.rem(t, per_chunk)

        @pl.when((c < n_chunks) & (tc < gu_ticks))
        def _():
            gate_up(c, tc)

        @pl.when((c < n_chunks) & (tc >= gu_ticks))
        def _():
            down(c, tc - gu_ticks)

        for off, fn in reversed(tuple(zip(OFFSETS, stages))):
            e = t - FIRST - off
            u = lax.div(e, pace)

            @pl.when((e >= 0) & (lax.rem(e, pace) == 0) & (u < n_units))
            def _(u=u, fn=fn):
                fn(u)

        return carry

    lax.fori_loop(0, total, tick, 0)

    for u in (n_units - 2, n_units - 1):
        pair_copy(u).wait_send()

    def finish(u, carry):
        share_copy(u).wait()
        return carry

    lax.fori_loop(0, n_units, finish, 0)


def _mlp(mesh, chunk, ff_tile, x, w_gate, w_up, w_down):
    rows, d = x.shape
    ff = w_gate.shape[1]
    side = math.isqrt(mesh.shape[AXIS] // CORES)
    unit = d // UNITS
    tile = unit // TILES
    half_rows = chunk // CORES
    brows = half_rows // STREAMS // RING
    bcols = unit // RING
    n_units = rows // chunk * UNITS
    assert side == RING and side * side * CORES == mesh.shape[AXIS]
    assert 2 * (ff // ff_tile) + UNITS * TILES == UNITS * 5
    bf, dma = jnp.bfloat16, pltpu.SemaphoreType.DMA
    any_spec = pl.BlockSpec(memory_space=pl.ANY)
    return pl.pallas_call(
        functools.partial(_kernel, (side, rows, chunk, ff_tile, unit)),
        name="mlp_sum",
        out_shape=jax.ShapeDtypeStruct((rows, d), bf),
        in_specs=[any_spec] * 4,
        out_specs=any_spec,
        scratch_shapes=[
            pltpu.VMEM((chunk, d), bf),
            pltpu.VMEM((chunk, ff), bf),
            pltpu.VMEM((2, d, ff_tile), bf),
            pltpu.VMEM((2, d, ff_tile), bf),
            pltpu.VMEM((2, ff, tile), bf),
            pltpu.VMEM((SLOTS, half_rows, unit), jnp.float32),
            pltpu.VMEM((2, half_rows, unit), bf),
            pltpu.VMEM((SLOTS, half_rows, unit), bf),
            pltpu.VMEM((SLOTS, STREAMS, 6, brows, unit // 2), bf),
            pltpu.VMEM((SLOTS, STREAMS, 6, brows, unit // 2), bf),
            pltpu.VMEM((SLOTS, STREAMS, 6, brows, bcols // 2), bf),
            pltpu.VMEM((SLOTS, STREAMS, 6, brows, bcols // 2), bf),
            pltpu.VMEM((2, STREAMS, brows, unit), jnp.float32),
            pltpu.VMEM((SLOTS, STREAMS, brows, bcols), bf),
            dma((UNITS * TILES,)), dma((2,)), dma((2,)), dma((2,)),
            dma((2,)), dma((SLOTS,)),
            dma((SLOTS, STREAMS, 6)), dma((SLOTS, STREAMS, 6)),
            dma((SLOTS, STREAMS, 6)), dma((SLOTS, STREAMS, 6)),
            dma((SLOTS, STREAMS, 4)), dma((SLOTS, STREAMS, 4)),
            dma((SLOTS, STREAMS, 4)), dma((SLOTS, STREAMS, 4)),
            dma((SLOTS, STREAMS)), dma((n_units,)), dma((n_units,)),
            pltpu.SemaphoreType.REGULAR,
        ],
        compiler_params=pltpu.CompilerParams(
            collective_id=0, has_side_effects=True, vmem_limit_bytes=VMEM_LIMIT
        ),
        cost_estimate=pl.CostEstimate(
            flops=6 * rows * d * ff, bytes_accessed=3 * d * ff * 2 * (rows // chunk), transcendentals=rows * ff
        ),
    )(x, w_gate, w_up, w_down)


def solution(mesh):
    return jax.shard_map(
        functools.partial(_mlp, mesh, CHUNK, FF_TILE),
        mesh=mesh,
        in_specs=(P("dp", None), P(None, AXIS), P(None, AXIS), P(AXIS, None)),
        out_specs=P("dp", None),
        check_vma=False,
    )
```

time: 474 us -> 326 us (0.69)
  Pallas kernels: 0 us -> 303 us
  waiting for transfers between devices: 253 us -> 0 us
  matrix products: 184 us -> 0 us
  between operations: 13.4 us -> 0.01 us
    pallas_call x0 -> x1, Pallas kernels: none -> 303 us  [_mlp(): pl.pallas_call(functools.partial(_kernel, (side, rows, chunk, ff_tile, un...]
    psum x1 -> x0, waiting for transfers between devices: 253 us -> none  [step(): return lax.psum(term, 'tp')]
    dot_general x3 -> x0, matrix products: 184 us -> none  [the longest x1 63.4 us: step(): up = jnp.dot(x, w_up, preferred_element_type=jnp.float32)]
  transfers between devices with their start and end apart: 1 -> 0, of which waited for: 1 -> 0; matrix products, arithmetic and copies ran while one was open for 0% -> 0% of each run, Pallas kernels for 0% -> 0%
where the time goes in v1:
time: 326 us
  Pallas kernels  303 us (93%)
  local copies, waits for them, and re-layouts  23 us (7%)
    pallas_call x1, Pallas kernels, _mlp(): pl.pallas_call(functools.partial(_kernel, (side, rows, chunk, ff_tile, un...  303 us
    unnamed x1, local copies, waits for them, and re-layouts  23 us

profile of v1, /device:TPU:97, one launch (start us, length us, event | category | flops | bytes accessed | tf_op | source)
XLA Modules:
  0.0 325.8 jit_solution(3340651511457875943)
XLA Ops:
  0.0 302.8 %mlp_sum.1 = bf16[2048,8192]{1,0:T(8,128)(2,1)} custom-call(bf16[2048,8192]{1,0:T(8,128)(2,1)} %x_hbm.1, bf16[8192,1536]{1,0:T(8,128)(2,1)} %wg_hbm.1, bf16[8192,1536]{1,0:T(8,128)(2,1)} %wu_hbm.1, bf16[1536,8192]{1,0:T(8,128)(2,1)} %wd_hbm.1), custom_call_target="tpu_custom_call" | custom-call | flops 154618822656 | bytes 301989888 | tf_op jit(solution)/shard_map/mlp_sum/pallas_call | solution.py:386
  302.8 23.0 %copy.6 = bf16[2048,8192]{1,0:T(8,128)(2,1)} copy(bf16[2048,8192]{1,0:T(8,128)(2,1)} %mlp_sum.1) | data formatting | bytes 67108864

commit v2 on v1

--- a/solution.py
+++ b/solution.py
@@ -14,11 +14,13 @@
 STREAMS = 2
 CHUNK = 512
 FF_TILE = 256
-UNITS = 4
-TILES = 2
-SLOTS = 4
-FIRST = 15
-OFFSETS = (0, 3, 5, 7, 9, 11, 13, 16, 18)
+UNITS = 8
+TILES = 1
+SLOTS = 8
+GATHERS = 16
+FIRST = 14
+STEP = 1
+OFFSETS = (0, 2, 4, 6, 8, 10, 12, 15, 17)
 VMEM_LIMIT = 67_043_328
 
 
@@ -35,7 +37,6 @@
     gu_ticks = 2 * n_ff
     down_ticks = UNITS * TILES
     per_chunk = gu_ticks + down_ticks
-    pace = per_chunk // UNITS
     tile = unit // TILES
     half_rows = chunk // CORES
     srows = half_rows // STREAMS
@@ -93,13 +94,27 @@
         ps, s = lax.rem(u, 2), lax.rem(u, SLOTS)
         return remote(psend.at[ps], precv.at[s], pair_ss.at[ps], pair_rs.at[s], partner)
 
+    def ring_refs(ring):
+        return (s1, r1, s1_ss, s1_rs, ring1) if ring == 1 else (s2, r2, s2_ss, s2_rs, ring2)
+
     def rs_copy(ring, u, st, k):
         s = lax.rem(u, SLOTS)
-        if ring == 1:
-            sb, rb, ss, rs, nb = s1, r1, s1_ss, s1_rs, ring1
-        else:
-            sb, rb, ss, rs, nb = s2, r2, s2_ss, s2_rs, ring2
-        return remote(sb.at[s, st, k], rb.at[s, st, k], ss.at[s, st, k], rs.at[s, st, k], nb[st][k % 2])
+        sb, rb, ss, rs, nb = ring_refs(ring)
+        part = pl.ds(2 * k, 2) if k < 2 else k + 2
+        return remote(sb.at[s, st, part], rb.at[s, st, part], ss.at[s], rs.at[s, k // 2], nb[st][k % 2])
+
+    def landed(ref, sem):
+        pltpu.make_async_copy(ref, ref, sem).wait()
+
+    def rs_landed(ring, u, step):
+        s = lax.rem(u, SLOTS)
+        _, rb, _, rs, _ = ring_refs(ring)
+        landed(rb.at[s, :, pl.ds(4 * step, 4 - 2 * step)], rs.at[s, step])
+
+    def rs_sent(ring, u):
+        s = lax.rem(u, SLOTS)
+        sb, _, ss, _, _ = ring_refs(ring)
+        landed(sb.at[s], ss.at[s])
 
     def y_rows(u, st, q):
         base = lax.div(u, UNITS) * chunk + core * half_rows + st * srows + q * brows
@@ -109,7 +124,7 @@
         return pl.ds(pl.multiple_of(lax.rem(u, UNITS) * unit + off, width), width)
 
     def ag2_copy(u, st, k):
-        s = lax.rem(u, SLOTS)
+        s = lax.rem(u, GATHERS)
         p1, p2 = pos1[st], pos2[st]
         if k < 2:
             dst = y_hbm.at[y_rows(u, st, p1), y_cols(u, p2 * bcols, bcols)]
@@ -117,15 +132,15 @@
         else:
             off = prv(p2) * bcols if k == 2 else nxt(p2) * bcols + h2
             src = dst = y_hbm.at[y_rows(u, st, p1), y_cols(u, off, h2)]
-        return remote(src, dst, g2_ss.at[s, st, k], g2_rs.at[s, st, k], ring2[st][k % 2])
+        return remote(src, dst, g2_ss.at[s], g2_rs.at[s, k // 2], ring2[st][k % 2])
 
     def loc_copy(u, st):
-        s = lax.rem(u, SLOTS)
+        s = lax.rem(u, GATHERS)
         dst = y_hbm.at[y_rows(u, st, pos1[st]), y_cols(u, pos2[st] * bcols, bcols)]
-        return pltpu.make_async_copy(fin.at[s, st], dst, loc_sem.at[s, st])
+        return pltpu.make_async_copy(fin.at[s, st], dst, loc_sem.at[s])
 
     def ag1_copy(u, st, k):
-        s = lax.rem(u, SLOTS)
+        s = lax.rem(u, GATHERS)
         p1 = pos1[st]
         if k < 2:
             part = y_hbm.at[y_rows(u, st, p1), y_cols(u, 0, unit)]
@@ -133,7 +148,18 @@
             part = y_hbm.at[y_rows(u, st, prv(p1)), y_cols(u, 0, h1)]
         else:
             part = y_hbm.at[y_rows(u, st, nxt(p1)), y_cols(u, h1, h1)]
-        return remote(part, part, g1_ss.at[s, st, k], g1_rs.at[s, st, k], ring1[st][k % 2])
+        return remote(part, part, g1_ss.at[s], g1_rs.at[s, k // 2], ring1[st][k % 2])
+
+    def ag_landed(ring, u, step):
+        s = lax.rem(u, GATHERS)
+        rows_, cols_ = (brows, unit) if ring == 2 else (brows * RING, unit)
+        part = y_hbm.at[pl.ds(0, rows_ // (1 + step)), pl.ds(0, cols_)]
+        landed(part, (g1_rs if ring == 1 else g2_rs).at[s, step])
+
+    def ag_sent(u):
+        s = lax.rem(u, GATHERS)
+        for sem, n in ((g2_ss, brows), (g1_ss, brows * RING)):
+            landed(y_hbm.at[pl.ds(0, n + n // 2), pl.ds(0, unit)], sem.at[s])
 
     def share_copy(u):
         base = lax.div(u, UNITS) * chunk + core * half_rows
@@ -147,119 +173,102 @@
     def rows_of(st, q):
         return pl.ds(pl.multiple_of(st * srows + q * brows, brows), brows)
 
+    def chip_sum(s, st, q, cols):
+        r = rows_of(st, q)
+        return own[s, r, cols] + f32(precv[s, r, cols])
+
+    def f1_half(u, st, q, off):
+        return f1[lax.rem(u, SLOTS), st, :, pl.ds(pl.multiple_of(q * bcols + off, h2), h2)]
+
     def stage_pair(u):
         s = lax.rem(u, SLOTS)
         pair_copy(u).wait_recv()
         for st in range(STREAMS):
             p = pos1[st]
-            for d, cols, k in (
-                (2, A1, 0), (2, B1, 1), (1, B1, 2), (3, A1, 3),
-                (1, A1, None), (3, B1, None), (0, A1, None), (0, B1, None),
-            ):
-                r = rows_of(st, lax.rem(p + d, side))
-                v = own[s, r, cols] + f32(precv[s, r, cols])
-                if k is None:
-                    own[s, r, cols] = v
-                else:
-                    s1[s, st, k] = b16(v)
-        for k in range(4):
+            for d, cols, k in ((2, A1, 0), (1, B1, 1), (2, B1, 2), (3, A1, 3)):
+                s1[s, st, k] = b16(chip_sum(s, st, lax.rem(p + d, side), cols))
+        for k in range(2):
             for st in range(STREAMS):
                 rs_copy(1, u, st, k).start()
 
-        @pl.when(u + SLOTS < n_units)
-        def _():
-            pl.semaphore_signal(credit, inc=1, device_id={AXIS: partner}, device_id_type=pl.DeviceIdType.MESH)
-
     def stage_rs1_fwd(u):
         s = lax.rem(u, SLOTS)
+        rs_landed(1, u, 0)
         for st in range(STREAMS):
             p = pos1[st]
-            rs_copy(1, u, st, 0).wait_recv()
-            s1[s, st, 4] = b16(own[s, rows_of(st, nxt(p)), A1] + f32(r1[s, st, 0]))
-            rs_copy(1, u, st, 1).wait_recv()
-            s1[s, st, 5] = b16(own[s, rows_of(st, prv(p)), B1] + f32(r1[s, st, 1]))
-        for k in (4, 5):
+            s1[s, st, 4] = b16(chip_sum(s, st, nxt(p), A1) + f32(r1[s, st, 0]))
+            s1[s, st, 5] = b16(chip_sum(s, st, prv(p), B1) + f32(r1[s, st, 2]))
+        for k in (2, 3):
             for st in range(STREAMS):
                 rs_copy(1, u, st, k).start()
 
     def stage_rs1_end(u):
         s = lax.rem(u, SLOTS)
-        fs = lax.rem(u, 2)
-        for st in range(STREAMS):
-            r = rows_of(st, pos1[st])
-            for k in (3, 4, 2, 5):
-                rs_copy(1, u, st, k).wait_recv()
-            f1[fs, st, :, A1] = own[s, r, A1] + f32(r1[s, st, 3]) + f32(r1[s, st, 4])
-            f1[fs, st, :, B1] = own[s, r, B1] + f32(r1[s, st, 2]) + f32(r1[s, st, 5])
-            for d, off, k in ((2, 0, 0), (2, h2, 1), (1, h2, 2), (3, 0, 3)):
-                q = lax.rem(pos2[st] + d, side)
-                s2[s, st, k] = b16(f1[fs, st, :, pl.ds(pl.multiple_of(q * bcols + off, h2), h2)])
-        for k in range(4):
+        rs_landed(1, u, 1)
+        for st in range(STREAMS):
+            p = pos1[st]
+            f1[s, st, :, A1] = chip_sum(s, st, p, A1) + f32(r1[s, st, 3]) + f32(r1[s, st, 4])
+            f1[s, st, :, B1] = chip_sum(s, st, p, B1) + f32(r1[s, st, 1]) + f32(r1[s, st, 5])
+            for d, off, k in ((2, 0, 0), (1, h2, 1), (2, h2, 2), (3, 0, 3)):
+                s2[s, st, k] = b16(f1_half(u, st, lax.rem(pos2[st] + d, side), off))
+        for k in range(2):
             for st in range(STREAMS):
                 rs_copy(2, u, st, k).start()
 
-    def f1_half(u, st, q, off):
-        return f1[lax.rem(u, 2), st, :, pl.ds(pl.multiple_of(q * bcols + off, h2), h2)]
+        @pl.when(u + SLOTS < n_units)
+        def _():
+            pl.semaphore_signal(credit, inc=1, device_id={AXIS: partner}, device_id_type=pl.DeviceIdType.MESH)
 
     def stage_rs2_fwd(u):
         s = lax.rem(u, SLOTS)
+        rs_landed(2, u, 0)
         for st in range(STREAMS):
             p = pos2[st]
-            rs_copy(2, u, st, 0).wait_recv()
             s2[s, st, 4] = b16(f1_half(u, st, nxt(p), 0) + f32(r2[s, st, 0]))
-            rs_copy(2, u, st, 1).wait_recv()
-            s2[s, st, 5] = b16(f1_half(u, st, prv(p), h2) + f32(r2[s, st, 1]))
-        for k in (4, 5):
+            s2[s, st, 5] = b16(f1_half(u, st, prv(p), h2) + f32(r2[s, st, 2]))
+        for k in (2, 3):
             for st in range(STREAMS):
                 rs_copy(2, u, st, k).start()
 
     def stage_rs2_end(u):
-        s = lax.rem(u, SLOTS)
+        s, gs = lax.rem(u, SLOTS), lax.rem(u, GATHERS)
+        rs_landed(2, u, 1)
         for st in range(STREAMS):
             p = pos2[st]
-            for k in (3, 4, 2, 5):
-                rs_copy(2, u, st, k).wait_recv()
             a = f1_half(u, st, p, 0) + f32(r2[s, st, 3]) + f32(r2[s, st, 4])
-            b = f1_half(u, st, p, h2) + f32(r2[s, st, 2]) + f32(r2[s, st, 5])
-            fin[s, st, :, pl.ds(0, h2)] = b16(a)
-            fin[s, st, :, pl.ds(h2, h2)] = b16(b)
+            b = f1_half(u, st, p, h2) + f32(r2[s, st, 1]) + f32(r2[s, st, 5])
+            fin[gs, st, :, pl.ds(0, h2)] = b16(a)
+            fin[gs, st, :, pl.ds(h2, h2)] = b16(b)
         for st in range(STREAMS):
             for k in range(2):
                 ag2_copy(u, st, k).start()
             loc_copy(u, st).start()
+        rs_sent(1, u)
 
     def stage_ag2_fwd(u):
-        for st in range(STREAMS):
-            for k in range(2):
-                ag2_copy(u, st, k).wait_recv()
-                ag2_copy(u, st, k + 2).start()
+        ag_landed(2, u, 0)
+        for st in range(STREAMS):
+            for k in (2, 3):
+                ag2_copy(u, st, k).start()
 
     def stage_ag1(u):
-        for st in range(STREAMS):
-            loc_copy(u, st).wait()
-            for k in (2, 3):
-                ag2_copy(u, st, k).wait_recv()
+        landed(fin.at[lax.rem(u, GATHERS)], loc_sem.at[lax.rem(u, GATHERS)])
+        ag_landed(2, u, 1)
+        for st in range(STREAMS):
             for k in range(2):
                 ag1_copy(u, st, k).start()
+        rs_sent(2, u)
 
     def stage_ag1_fwd(u):
-        for st in range(STREAMS):
-            for k in range(2):
-                ag1_copy(u, st, k).wait_recv()
-                ag1_copy(u, st, k + 2).start()
+        ag_landed(1, u, 0)
+        for st in range(STREAMS):
+            for k in (2, 3):
+                ag1_copy(u, st, k).start()
 
     def stage_share(u):
-        for st in range(STREAMS):
-            for k in (2, 3):
-                ag1_copy(u, st, k).wait_recv()
+        ag_landed(1, u, 1)
         share_copy(u).start()
-        for st in range(STREAMS):
-            for k in range(6):
-                rs_copy(1, u, st, k).wait_send()
-                rs_copy(2, u, st, k).wait_send()
-            for k in range(4):
-                ag2_copy(u, st, k).wait_send()
-                ag1_copy(u, st, k).wait_send()
+        ag_sent(u)
 
     stages = (
         stage_pair, stage_rs1_fwd, stage_rs1_end, stage_rs2_fwd, stage_rs2_end,
@@ -334,7 +343,7 @@
         x_copy(0, i).start()
     wd_copy(0).start()
 
-    total = (n_units - 1) * pace + FIRST + OFFSETS[-1] + 1
+    total = (n_chunks - 1) * per_chunk + (UNITS - 1) * STEP + FIRST + OFFSETS[-1] + 1
 
     def tick(t, carry):
         c, tc = lax.div(t, per_chunk), lax.rem(t, per_chunk)
@@ -347,11 +356,12 @@
         def _():
             down(c, tc - gu_ticks)
 
-        for off, fn in reversed(tuple(zip(OFFSETS, stages))):
+        for off, fn in zip(OFFSETS, stages):
             e = t - FIRST - off
-            u = lax.div(e, pace)
-
-            @pl.when((e >= 0) & (lax.rem(e, pace) == 0) & (u < n_units))
+            j = lax.rem(e, per_chunk)
+            u = lax.div(e, per_chunk) * UNITS + lax.div(j, STEP)
+
+            @pl.when((e >= 0) & (lax.rem(j, STEP) == 0) & (j < UNITS * STEP) & (u < n_units))
             def _(u=u, fn=fn):
                 fn(u)
 
@@ -380,7 +390,7 @@
     bcols = unit // RING
     n_units = rows // chunk * UNITS
     assert side == RING and side * side * CORES == mesh.shape[AXIS]
-    assert 2 * (ff // ff_tile) + UNITS * TILES == UNITS * 5
+    assert 2 * (ff // ff_tile) + UNITS * TILES == 5 * UNITS * TILES // 2
     bf, dma = jnp.bfloat16, pltpu.SemaphoreType.DMA
     any_spec = pl.BlockSpec(memory_space=pl.ANY)
     return pl.pallas_call(
@@ -402,15 +412,13 @@
             pltpu.VMEM((SLOTS, STREAMS, 6, brows, unit // 2), bf),
             pltpu.VMEM((SLOTS, STREAMS, 6, brows, bcols // 2), bf),
             pltpu.VMEM((SLOTS, STREAMS, 6, brows, bcols // 2), bf),
-            pltpu.VMEM((2, STREAMS, brows, unit), jnp.float32),
-            pltpu.VMEM((SLOTS, STREAMS, brows, bcols), bf),
+            pltpu.VMEM((SLOTS, STREAMS, brows, unit), jnp.float32),
+            pltpu.VMEM((GATHERS, STREAMS, brows, bcols), bf),
             dma((UNITS * TILES,)), dma((2,)), dma((2,)), dma((2,)),
             dma((2,)), dma((SLOTS,)),
-            dma((SLOTS, STREAMS, 6)), dma((SLOTS, STREAMS, 6)),
-            dma((SLOTS, STREAMS, 6)), dma((SLOTS, STREAMS, 6)),
-            dma((SLOTS, STREAMS, 4)), dma((SLOTS, STREAMS, 4)),
-            dma((SLOTS, STREAMS, 4)), dma((SLOTS, STREAMS, 4)),
-            dma((SLOTS, STREAMS)), dma((n_units,)), dma((n_units,)),
+            dma((SLOTS,)), dma((SLOTS, 2)), dma((SLOTS,)), dma((SLOTS, 2)),
+            dma((GATHERS,)), dma((GATHERS, 2)), dma((GATHERS,)), dma((GATHERS, 2)),
+            dma((GATHERS,)), dma((n_units,)), dma((n_units,)),
             pltpu.SemaphoreType.REGULAR,
         ],
         compiler_params=pltpu.CompilerParams(

time: 326 us -> 288 us (0.88)
  Pallas kernels: 303 us -> 265 us
    pallas_call x1, Pallas kernels: 303 us -> 265 us  [_mlp(): pl.pallas_call(functools.partial(_kernel, (side, rows, chunk, ff_tile, un...]
where the time goes in v2:
time: 288 us
  Pallas kernels  265 us (92%)
  local copies, waits for them, and re-layouts  23 us (8%)
    pallas_call x1, Pallas kernels, _mlp(): pl.pallas_call(functools.partial(_kernel, (side, rows, chunk, ff_tile, un...  265 us
    unnamed x1, local copies, waits for them, and re-layouts  23 us

profile of v2, /device:TPU:97, one launch (start us, length us, event | category | flops | bytes accessed | tf_op | source)
XLA Modules:
  0.0 287.9 jit_solution(4964186137685226744)
XLA Ops:
  0.0 264.9 %mlp_sum.1 = bf16[2048,8192]{1,0:T(8,128)(2,1)} custom-call(bf16[2048,8192]{1,0:T(8,128)(2,1)} %x_hbm.1, bf16[8192,1536]{1,0:T(8,128)(2,1)} %wg_hbm.1, bf16[8192,1536]{1,0:T(8,128)(2,1)} %wu_hbm.1, bf16[1536,8192]{1,0:T(8,128)(2,1)} %wd_hbm.1), custom_call_target="tpu_custom_call" | custom-call | flops 154618822656 | bytes 301989888 | tf_op jit(solution)/shard_map/mlp_sum/pallas_call | solution.py:396
  264.9 23.0 %copy.6 = bf16[2048,8192]{1,0:T(8,128)(2,1)} copy(bf16[2048,8192]{1,0:T(8,128)(2,1)} %mlp_sum.1) | data formatting | bytes 67108864
